TPU v7x, 32 devices: a 4x4x1 block of a 4x4x8 slice. The times are simulated.
32 devices in a mesh: rep: 2 (over z, core), dp: 16 (over x, y).
Axes of the slice: x: 4, y: 4, z: 1, core: 2. Of those that a mesh axis runs over, the one named last changes fastest.
The devices are a block of a 4x4x8 slice.
Arguments:
- x: bfloat16 [32, 4096, 512], P(('rep', 'dp')), parts along dimension 0
- dy: bfloat16 [32, 4096, 512], P(('rep', 'dp')), parts along dimension 0
- w_gate: bfloat16 [2, 512, 2048], P(None, 'dp')
- w_up: bfloat16 [2, 512, 2048], P(None, 'dp')
- w_down: bfloat16 [2, 2048, 512], P(None, 'dp')
Outputs:
- output 1: bfloat16 [32, 4096, 512], P(('rep', 'dp')), parts along dimension 0
- output 2: bfloat16 [4, 512, 2048], P('rep', 'dp'), parts along dimension 0
- output 3: bfloat16 [4, 512, 2048], P('rep', 'dp'), parts along dimension 0
- output 4: bfloat16 [4, 2048, 512], P('rep', 'dp'), parts along dimension 0
There are 2 independent parts. A program takes and returns all parts, laid end to end along the dimension named above; an argument that names none is the same for every part.
All inputs are finite; a program needn't handle non-finite values.
Results may differ from a plain program's by a relative error of at most 0.018.
Values are sent between devices in bfloat16 or wider.
A program may use at most 768 MiB of HBM per device.

v0:
```python
import jax
import jax.numpy as jnp
from jax import lax

NAMES = ("w_gate", "w_up", "w_down")


def matmul(a, w):
    return jnp.dot(a, w, preferred_element_type=jnp.float32).astype(jnp.bfloat16)


def normed(h):
    wide = h.astype(jnp.float32)
    scale = lax.rsqrt(jnp.mean(wide**2, -1, keepdims=True) + 1e-6)
    return (wide * scale).astype(jnp.bfloat16)


def layer(h, w):
    a = normed(h)
    gate = jnp.dot(a, w["w_gate"], preferred_element_type=jnp.float32)
    up = jnp.dot(a, w["w_up"], preferred_element_type=jnp.float32)
    return h + matmul((jax.nn.silu(gate) * up).astype(jnp.bfloat16), w["w_down"])


def stack(weights, h):
    for number in range(weights["w_gate"].shape[0]):
        h = layer(h, {name: w[number] for name, w in weights.items()})
    return h


def solution(mesh):
    groups = mesh.shape["rep"]

    def step(x, dy, *weights):
        shape = x.shape
        x, dy = (t.reshape(groups, -1, *t.shape[1:]) for t in (x, dy))

        def of_a_group(x, dy):
            _, back = jax.vjp(stack, dict(zip(NAMES, weights, strict=True)), x)
            by_weights, by_x = back(dy)
            return (by_x, *(by_weights[name] for name in NAMES))

        by_x, *by_weights = jax.vmap(of_a_group)(x, dy)
        return (by_x.reshape(shape), *(t.reshape(-1, *t.shape[2:]) for t in by_weights))

    return step
```

profile of v0, /device:TPU:98, one launch (start us, length us, event | category | flops | bytes accessed | tf_op | source)
XLA Modules:
  0.0 794.9 jit_solution(13780931592593621652)
XLA Ops:
  31.0 21.4 %all-gather.30.cloned.1.call-done = bf16[1,512,2048]{2,1,0:T(8,128)(2,1)} async-done(((bf16[1,32,2048]{2,1,0:T(8,128)(2,1)}), bf16[1,512,2048]{2,1,0:T(8,128)(2,1)}) %all-gather.30.cloned.1.call-update) | async-done | bytes 2097168 | tf_op jit(solution)/vmap(jvp())/squeeze | solution.py:27
  52.4 17.9 %fusion.113 = f32[4096,2048]{1,0:T(8,128)} fusion(bf16[1,512,2048]{2,1,0:T(8,128)(2,1)} %all-gather.30.cloned.1.call-done, bf16[1,4096,512]{2,1,0:T(8,128)(2,1)} %param.1, f32[4096]{0:T(1024)S(1)} %get-tuple-element.13), kind=kOutput, calls=%fused_computation.107 | convolution fusion | flops 8596226048 | bytes 39862272 | tf_op jit(solution)/vmap(jvp())/dot_general | solution.py:20
  70.3 23.7 %all-gather.32.cloned.1.call-done = bf16[1,512,2048]{2,1,0:T(8,128)(2,1)} async-done(((bf16[1,32,2048]{2,1,0:T(8,128)(2,1)}), bf16[1,512,2048]{2,1,0:T(8,128)(2,1)}) %all-gather.32.cloned.1.call-update) | async-done | bytes 2097168 | tf_op jit(solution)/vmap(jvp())/squeeze | solution.py:27
  94.0 17.8 %fusion.110 = f32[4096,2048]{1,0:T(8,128)} fusion(bf16[1,512,2048]{2,1,0:T(8,128)(2,1)} %all-gather.32.cloned.1.call-done, bf16[1,4096,512]{2,1,0:T(8,128)(2,1)} %param.1, f32[4096]{0:T(1024)S(1)} %get-tuple-element.13), kind=kOutput, calls=%fused_computation.104 | convolution fusion | flops 8596226048 | bytes 39862272 | tf_op jit(solution)/vmap(jvp())/dot_general | solution.py:21
  111.8 27.6 %fusion.24 = bf16[4096,2048]{1,0:T(8,128)(2,1)} fusion(f32[4096,2048]{1,0:T(8,128)} %fusion.110, f32[4096,2048]{1,0:T(8,128)} %fusion.113), kind=kLoop, calls=%fused_computation.34 | loop fusion | flops 50331648 | bytes 83886080
  139.4 16.3 %fusion.40 = (f32[4096]{0:T(1024)S(1)}, bf16[1,1,4096,512]{2,3,1,0:T(8,128)(2,1)}) fusion(bf16[4096,2048]{1,0:T(8,128)(2,1)} %fusion.24, bf16[1,2048,512]{2,1,0:T(8,128)(2,1)} %all-gather.34.cloned.1.call-done, bf16[1,4096,512]{1,2,0:T(8,128)(2,1)} %copy.1), kind=kOutput, calls=%fused_computation.62 | convolution fusion | flops 8600416256 | bytes 27279360 | tf_op jit(solution)/vmap(jvp())/dot_general | solution.py:9
  156.3 20.2 %all-gather.36.cloned.1.call-done = bf16[1,512,2048]{2,1,0:T(8,128)(2,1)} async-done(((bf16[1,32,2048]{2,1,0:T(8,128)(2,1)}), bf16[1,512,2048]{2,1,0:T(8,128)(2,1)}) %all-gather.36.cloned.1.call-update) | async-done | bytes 2097168 | tf_op jit(solution)/vmap(jvp())/squeeze | solution.py:27
  176.5 17.8 %fusion.100 = f32[4096,2048]{1,0:T(8,128)} fusion(bf16[1,1,4096,512]{2,3,1,0:T(8,128)(2,1)} %get-tuple-element.15, f32[4096]{0:T(1024)S(1)} %bitcast.314, bf16[1,512,2048]{2,1,0:T(8,128)(2,1)} %all-gather.36.cloned.1.call-done), kind=kOutput, calls=%fused_computation.95 | convolution fusion | flops 8596226048 | bytes 39862272 | tf_op jit(solution)/vmap(jvp())/dot_general | solution.py:20
  194.3 23.6 %all-gather.40.cloned.1.call-done = bf16[1,512,2048]{2,1,0:T(8,128)(2,1)} async-done(((bf16[1,32,2048]{2,1,0:T(8,128)(2,1)}), bf16[1,512,2048]{2,1,0:T(8,128)(2,1)}) %all-gather.40.cloned.1.call-update) | async-done | bytes 2097168 | tf_op jit(solution)/vmap(jvp())/squeeze | solution.py:27
  217.9 18.1 %fusion.98 = f32[4096,2048]{1,0:T(8,128)} fusion(bf16[1,1,4096,512]{2,3,1,0:T(8,128)(2,1)} %get-tuple-element.15, f32[4096]{0:T(1024)S(1)} %bitcast.315, bf16[1,512,2048]{2,1,0:T(8,128)(2,1)} %all-gather.40.cloned.1.call-done), kind=kOutput, calls=%fused_computation.94 | convolution fusion | flops 8596226048 | bytes 39862272 | tf_op jit(solution)/vmap(jvp())/dot_general | solution.py:21
  236.0 25.4 %fusion.88 = f32[1,2048,512]{2,1,0:T(8,128)} fusion(bf16[1,4096,512]{2,1,0:T(8,128)(2,1)S(1)} %copy-done.2, f32[4096,2048]{1,0:T(8,128)} %fusion.98, f32[4096,2048]{1,0:T(8,128)} %fusion.100), kind=kOutput, calls=%fused_computation.92 | convolution fusion | flops 8640266240 | bytes 75497472 | tf_op jit(solution)/vmap(transpose(jvp()))/dot_general | solution.py:9
  261.6 15.2 %convolution_convert_fusion.1 = bf16[4096,2048]{1,0:T(8,128)(2,1)} fusion(bf16[1,4096,512]{2,1,0:T(8,128)(2,1)} %param, bf16[1,2048,512]{2,1,0:T(8,128)(2,1)} %all-gather.38.cloned.1.call-done), kind=kOutput, calls=%fused_computation.42 | convolution fusion | flops 8598323200 | bytes 23068672 | tf_op jit(solution)/vmap(transpose(jvp()))/dot_general | solution.py:9
  276.8 27.1 %fusion.4 = bf16[4096,2048]{1,0:T(8,128)(2,1)S(1)} fusion(f32[4096,2048]{1,0:T(8,128)} %fusion.100, f32[4096,2048]{1,0:T(8,128)} %fusion.98, bf16[4096,2048]{1,0:T(8,128)(2,1)} %convolution_convert_fusion.1), kind=kLoop, calls=%fused_computation.10 | loop fusion | flops 100663296 | bytes 100663296
  320.0 24.3 %fusion.42 = (f32[4096]{0:T(1024)S(1)}, bf16[1,1,4096,512]{2,3,1,0:T(8,128)(2,1)}) fusion(bf16[1,1,4096,512]{2,3,1,0:T(8,128)(2,1)} %get-tuple-element.15, bf16[4096,512]{0,1:T(8,128)(2,1)} %convolution_convert_fusion.3, bf16[1,512,2048]{2,1,0:T(8,128)(2,1)S(1)} %copy-done.12, bf16[4096,2048]{1,0:T(8,128)(2,1)} %convolution_convert_fusion.1, ...), kind=kOutput, calls=%fused_computation.64 | convolution fusion | flops 8652845056 | bytes 65028096 | tf_op jit(solution)/vmap(transpose(jvp()))/dot_general | solution.py:21
  377.2 32.8 %fusion.7 = bf16[4096,2048]{1,0:T(8,128)(2,1)} fusion(f32[4096,2048]{1,0:T(8,128)} %fusion.113, f32[4096,2048]{1,0:T(8,128)} %fusion.110, bf16[4096,2048]{1,0:T(8,128)(2,1)} %convolution_convert_fusion), kind=kLoop, calls=%fused_computation.13 | loop fusion | flops 100663296 | bytes 100663296
  410.1 23.1 %fusion.77 = f32[1,512,2048]{2,1,0:T(8,128)} fusion(bf16[4096,2048]{1,0:T(8,128)(2,1)} %convolution_convert_fusion.1, f32[4096,2048]{1,0:T(8,128)} %fusion.100, bf16[1,1,4096,512]{2,3,1,0:T(8,128)(2,1)} %get-tuple-element.15, f32[4096]{0:T(1024)S(1)} %bitcast.317), kind=kOutput, calls=%fused_computation.88 | convolution fusion | flops 8646557696 | bytes 58736640 | tf_op jit(solution)/vmap(transpose(jvp()))/dot_general | solution.py:21
  447.3 24.4 %fusion.38 = (f32[4096]{0:T(1024)S(1)}, bf16[1,1,4096,512]{2,3,1,0:T(8,128)(2,1)}) fusion(bf16[1,4096,512]{1,2,0:T(8,128)(2,1)} %copy.1, bf16[4096,512]{0,1:T(8,128)(2,1)} %convolution_convert_fusion.2, bf16[1,512,2048]{2,1,0:T(8,128)(2,1)} %all-gather.32.cloned.1.call-done, bf16[4096,2048]{1,0:T(8,128)(2,1)} %convolution_convert_fusion, ...), kind=kOutput, calls=%fused_computation.60 | convolution fusion | flops 8652845056 | bytes 65028096 | tf_op jit(solution)/vmap(transpose(jvp()))/dot_general | solution.py:21
  471.8 23.0 %fusion.80 = f32[1,512,2048]{2,1,0:T(8,128)} fusion(bf16[4096,2048]{1,0:T(8,128)(2,1)} %convolution_convert_fusion, f32[4096,2048]{1,0:T(8,128)} %fusion.113, bf16[1,4096,512]{1,2,0:T(8,128)(2,1)} %copy.1, f32[4096]{0:T(1024)S(1)} %bitcast.319), kind=kOutput, calls=%fused_computation.89 | convolution fusion | flops 8646557696 | bytes 58736640 | tf_op jit(solution)/vmap(transpose(jvp()))/dot_general | solution.py:21
  495.0 15.2 %convolution_bitcast_fusion = f32[1,512,2048]{2,1,0:T(8,128)} fusion(bf16[4096,2048]{1,0:T(8,128)(2,1)} %copy-done, bf16[1,1,4096,512]{2,3,1,0:T(8,128)(2,1)} %get-tuple-element.15, f32[4096]{0:T(1024)S(1)} %bitcast.318), kind=kOutput, calls=%fused_computation.90 | convolution fusion | flops 8596226048 | bytes 25182208 | tf_op jit(solution)/vmap(transpose(jvp()))/dot_general | solution.py:20
  510.3 14.9 %fusion.93 = f32[1,512,2048]{2,1,0:T(8,128)} fusion(bf16[4096,2048]{1,0:T(8,128)(2,1)} %fusion.7, bf16[1,4096,512]{1,2,0:T(8,128)(2,1)} %copy.1, f32[4096]{0:T(1024)S(1)} %bitcast.320), kind=kOutput, calls=%fused_computation.93 | convolution fusion | flops 8596226048 | bytes 25182208 | tf_op jit(solution)/vmap(transpose(jvp()))/dot_general | solution.py:20
  542.0 16.7 %reduce-scatter.23.cloned.1.call-done = f32[1,32,2048]{2,1,0:T(8,128)} async-done(((f32[1,512,2048]{2,1,0:T(8,128)}), f32[1,32,2048]{2,1,0:T(8,128)}) %reduce-scatter.23.cloned.1.call-update) | async-done | bytes 262160
  559.7 74.7 %reduce-scatter.25.cloned.1.call-done = f32[1,32,2048]{2,1,0:T(8,128)} async-done(((f32[1,512,2048]{2,1,0:T(8,128)}), f32[1,32,2048]{2,1,0:T(8,128)}) %reduce-scatter.25.cloned.1.call-update) | async-done | bytes 262160
  636.1 74.2 %reduce-scatter.19.cloned.1.call-done = f32[1,32,2048]{2,1,0:T(8,128)} async-done(((f32[1,512,2048]{2,1,0:T(8,128)}), f32[1,32,2048]{2,1,0:T(8,128)}) %reduce-scatter.19.cloned.1.call-update) | async-done | bytes 262160
  711.3 74.6 %reduce-scatter.21.cloned.1.call-done = f32[1,32,2048]{2,1,0:T(8,128)} async-done(((f32[1,512,2048]{2,1,0:T(8,128)}), f32[1,32,2048]{2,1,0:T(8,128)}) %reduce-scatter.21.cloned.1.call-update) | async-done | bytes 262160
  (81 shorter events, 110.0 us)
Async XLA Ops:
  7.2 45.2 %all-gather.30.cloned.1.call-start = ((), (), s32[]{:S(2)}) async-start(), calls=%async_computation.6 | async-start | bytes 2228224 | tf_op jit(solution)/vmap(jvp())/squeeze | solution.py:27
  9.0 85.0 %all-gather.32.cloned.1.call-start = ((), (), s32[]{:S(2)}) async-start(), calls=%async_computation.7 | async-start | bytes 2228224 | tf_op jit(solution)/vmap(jvp())/squeeze | solution.py:27
  10.8 128.6 %all-gather.34.cloned.1.call-start = ((), (), s32[]{:S(2)}) async-start(), calls=%async_computation.8 | async-start | bytes 2228224 | tf_op jit(solution)/vmap(jvp())/squeeze | solution.py:27
  12.6 163.9 %all-gather.36.cloned.1.call-start = ((), (), s32[]{:S(2)}) async-start(), calls=%async_computation.9 | async-start | bytes 2228224 | tf_op jit(solution)/vmap(jvp())/squeeze | solution.py:27
  13.2 204.7 %all-gather.40.cloned.1.call-start = ((), (), s32[]{:S(2)}) async-start(), calls=%async_computation.11 | async-start | bytes 2228224 | tf_op jit(solution)/vmap(jvp())/squeeze | solution.py:27
  13.9 247.7 %all-gather.38.cloned.1.call-start = ((), (), s32[]{:S(2)}) async-start(), calls=%async_computation.10 | async-start | bytes 2228224 | tf_op jit(solution)/vmap(jvp())/squeeze | solution.py:27
  14.5 524.7 %reduce-scatter.27.cloned.1.call-start = ((), (), s32[]{:S(2)}) async-start(), calls=%async_computation.16 | async-start | bytes 4456448
  156.3 61.6 %copy-start.6 = (f32[1,1,4096]{2,1,0:T(1,128)}, f32[1,1,4096]{2,1,0:T(1,128)S(1)}, u32[]{:S(2)}) copy-start(f32[1,1,4096]{2,1,0:T(1,128)S(1)} %rsqrt.23) | copy-start | bytes 49156
  217.9 18.1 %copy-start.2 = (bf16[1,4096,512]{2,1,0:T(8,128)(2,1)S(1)}, bf16[1,4096,512]{2,1,0:T(8,128)(2,1)}, u32[]{:S(2)}) copy-start(bf16[1,4096,512]{2,1,0:T(8,128)(2,1)} %param) | copy-start | bytes 12582916
  261.5 278.8 %reduce-scatter.29.cloned.1.call-start = ((), (), s32[]{:S(2)}) async-start(), calls=%async_computation.17 | async-start | bytes 4456448
  276.8 32.8 %copy-start.11 = (bf16[1,512,2048]{2,1,0:T(8,128)(2,1)S(1)}, bf16[1,512,2048]{2,1,0:T(8,128)(2,1)}, u32[]{:S(2)}) copy-start(bf16[1,512,2048]{2,1,0:T(8,128)(2,1)} %all-gather.36.cloned.1.call-done) | copy-start | bytes 6291460
  303.8 5.7 copy-start
  309.6 10.4 %copy-start.12 = (bf16[1,512,2048]{2,1,0:T(8,128)(2,1)S(1)}, bf16[1,512,2048]{2,1,0:T(8,128)(2,1)}, u32[]{:S(2)}) copy-start(bf16[1,512,2048]{2,1,0:T(8,128)(2,1)} %all-gather.40.cloned.1.call-done) | copy-start | bytes 6291460
  320.0 24.3 %copy-start.4 = (f32[4096]{0:T(1024)S(1)}, f32[4096]{0:T(1024)}, u32[]{:S(2)}) copy-start(f32[4096]{0:T(1024)} %copy-done.3) | copy-start | bytes 49156
  320.0 24.3 %copy-start.7 = (f32[1,1,4096]{2,1,0:T(1,128)S(1)}, f32[1,1,4096]{2,1,0:T(1,128)}, u32[]{:S(2)}) copy-start(f32[1,1,4096]{2,1,0:T(1,128)} %copy-done.6) | copy-start | bytes 49156
  344.3 6.4 copy-start.10
  350.7 12.5 %copy-start.1 = (bf16[1,1,4096,512]{2,3,1,0:T(8,128)(2,1)}, bf16[1,1,4096,512]{2,3,1,0:T(8,128)(2,1)S(1)}, u32[]{:S(2)}) copy-start(bf16[1,1,4096,512]{2,3,1,0:T(8,128)(2,1)S(1)} %fusion.67) | copy-start | bytes 12582916
  410.0 23.3 %copy-start.9 = (bf16[1,512,2048]{2,1,0:T(8,128)(2,1)S(1)}, bf16[1,512,2048]{2,1,0:T(8,128)(2,1)}, u32[]{:S(2)}) copy-start(bf16[1,512,2048]{2,1,0:T(8,128)(2,1)} %all-gather.30.cloned.1.call-done) | copy-start | bytes 6291460
  410.0 148.7 %reduce-scatter.23.cloned.1.call-start = ((), (), s32[]{:S(2)}) async-start(), calls=%async_computation.14 | async-start | bytes 4456448
  433.2 201.2 %reduce-scatter.25.cloned.1.call-start = ((), (), s32[]{:S(2)}) async-start(), calls=%async_computation.15 | async-start | bytes 4456448
  447.3 24.5 %copy-start.5 = (f32[4096]{0:T(1024)S(1)}, f32[4096]{0:T(1024)}, u32[]{:S(2)}) copy-start(f32[4096]{0:T(1024)} %get-tuple-element.12) | copy-start | bytes 49156
  471.8 23.2 %copy-start.8 = (f32[1,1,4096]{2,1,0:T(1,128)S(1)}, f32[1,1,4096]{2,1,0:T(1,128)}, u32[]{:S(2)}) copy-start(f32[1,1,4096]{2,1,0:T(1,128)} %copy-done.6) | copy-start | bytes 49156
  494.9 215.4 %reduce-scatter.19.cloned.1.call-start = ((), (), s32[]{:S(2)}) async-start(), calls=%async_computation.12 | async-start | bytes 4456448
  510.2 275.6 %reduce-scatter.21.cloned.1.call-start = ((), (), s32[]{:S(2)}) async-start(), calls=%async_computation.13 | async-start | bytes 4456448
  (1 other events, 0.6 us)
Sparse Core Ops, SparseCore 0:
  10.0 42.3 all-gather.29
  54.9 39.0 all-gather.31
  96.0 39.0 all-gather.33
  137.4 39.0 all-gather.35
  178.9 39.0 all-gather.39
  219.7 39.0 all-gather.37
  262.0 72.6 reduce-scatter.26
  410.1 72.6 reduce-scatter.28
  486.0 72.6 reduce-scatter.22
  561.7 72.6 reduce-scatter.24
  637.6 72.6 reduce-scatter.18
  713.3 72.5 reduce-scatter.20
where the time goes:
time: 804 us; the launch traced here: 795 us
  waiting for transfers between devices  331 us (41%)
  matrix products  304 us (38%)
  other arithmetic  113 us (14%)
  local copies, waits for them, and re-layouts  30.5 us (4%)
  between operations  14.8 us (2%)
    unnamed x18, waiting for transfers between devices  242 us
    dot_general x6, matrix products, layer(): up = jnp.dot(a, w['w_up'], preferred_element_type=jnp.float32)  131 us
    dot_general x6, matrix products, layer(): gate = jnp.dot(a, w['w_gate'], preferred_element_type=jnp.float32)  90.2 us
    squeeze x6, waiting for transfers between devices, stack(): h = layer(h, {name: w[number] for name, w in weights.items()})  88.9 us
    unnamed x3, other arithmetic  87.4 us
    dot_general x5, matrix products, matmul(): jnp.dot(a, w, preferred_element_type=jnp.float32).astype(jnp.bfloat16)  83.3 us
    unnamed x29, local copies, waits for them, and re-layouts  25.5 us
  transfers between devices with their start and end apart: 12, of which 8 were waited for; matrix products, arithmetic and copies ran while one was open for 55% of the time, Pallas kernels for 0%

commit v1 on v0

v1 whole, which is shorter than its diff:
```python
import functools
import math

import jax
import jax.numpy as jnp
from jax import lax
from jax.experimental import pallas as pl
from jax.experimental.pallas import tpu as pltpu
from jax.sharding import PartitionSpec as P

F32, BF16 = jnp.float32, jnp.bfloat16
CHUNKS = 4
TILES = 8
EPS = 1e-6
HALVES = 2


def dot(a, b, ca, cb):
    return lax.dot_general(a, b, (((ca,), (cb,)), ((), ())), preferred_element_type=F32)


def kernel(
    side, layers, x_hbm, dy_hbm, gate_own, up_own, down_hbm, dx_hbm, out_gate, out_up, out_down, kept_hbm,
    w, h, a, dh, acc, g, s_tile, kept, order, fin, st1, st2, st3, st4, rc1, rc2, rc3, rc4,
    load_sem, keep_sem, ag_send, ag_recv, rs_send, rs_recv,
):
    tokens, d = h.shape[1:]
    rows, hid = w.shape[4:]
    tile = tokens // TILES
    half, quarter = hid // 2, hid // 4
    units = layers * CHUNKS
    me = lax.axis_index("dp")
    px, py = me // side, me % side
    xs = {k: (px + k + side) % side for k in (-1, 0, 1, 2)}
    ys = {k: (py + k + side) % side for k in (-1, 0, 1, 2)}
    beside = {
        ("x", 1): xs[1] * side + py,
        ("x", -1): xs[-1] * side + py,
        ("y", 1): px * side + ys[1],
        ("y", -1): px * side + ys[-1],
    }

    load_x = pltpu.make_async_copy(x_hbm, h.at[0], load_sem.at[0])
    load_dy = pltpu.make_async_copy(dy_hbm, dh, load_sem.at[1])
    load_w = pltpu.make_async_copy(down_hbm, w.at[:, 2, px, py], load_sem.at[2])
    load_w.start()
    load_x.start()
    load_dy.start()

    many = hid // (CHUNKS * rows)
    source = lax.broadcasted_iota(jnp.int32, (hid, hid), 0)
    goal = lax.broadcasted_iota(jnp.int32, (hid, hid), 1)
    chunk_of, place = goal // (many * rows), goal % (many * rows)
    at_source = (place // rows) * (CHUNKS * rows) + chunk_of * rows + place % rows
    order[...] = jnp.where(source == at_source, 1.0, 0.0).astype(BF16)
    run = many * rows
    owns = [(l, k, ref) for l in range(layers) for k, ref in enumerate((gate_own, up_own))]
    for q in range(CHUNKS):
        both = jnp.concatenate([ref[l, :, pl.ds(q * hid, hid)] for l, _, ref in owns], 0)
        moved = dot(both, order[...], 1, 0).astype(BF16)
        for n, (l, k, _) in enumerate(owns):
            for j in range(CHUNKS):
                piece = moved[n * rows : (n + 1) * rows, j * run : (j + 1) * run]
                w[l * CHUNKS + j, k, px, py, :, pl.ds(q * run, run)] = piece

    def finish(l):
        for q in range(CHUNKS):
            both = jnp.concatenate(
                [
                    jnp.concatenate([fin[j, k, :, pl.ds(q * run, run)] for j in range(CHUNKS)], 1)
                    for k in range(2)
                ],
                0,
            )
            moved = dot(both, order[...], 1, 1).astype(BF16)
            for k, ref in enumerate((out_gate, out_up)):
                ref[l, :, pl.ds(q * hid, hid)] = moved[k * rows : (k + 1) * rows]

    barrier = pltpu.get_barrier_semaphore()
    for target in beside.values():
        pl.semaphore_signal(barrier, inc=1, device_id={"dp": target})
    pl.semaphore_wait(barrier, len(beside))

    def gather_copies(u, s):
        copies = []
        for colour in range(2):
            axis = ("x", "y")[(colour + (s > 2)) % 2]
            for way, sign in ((0, 1), (1, -1)):
                lo = colour * half
                if s % 2:
                    lanes, at = pl.ds(lo, half), 0
                else:
                    lanes, at = pl.ds(lo + way * quarter, quarter), -sign
                pos = (xs if axis == "x" else ys)[at]
                if s <= 2:
                    i, j = (pos, py) if axis == "x" else (px, pos)
                else:
                    i, j = (pos, slice(None)) if axis == "x" else (slice(None), pos)
                ref = w.at[u, :, i, j, :, lanes]
                k = colour * 2 + way
                copies.append(
                    pltpu.make_async_remote_copy(
                        src_ref=ref,
                        dst_ref=ref,
                        send_sem=ag_send.at[u, s - 1, k],
                        recv_sem=ag_recv.at[u, s - 1, k],
                        device_id={"dp": beside[axis, sign]},
                    )
                )
        return copies

    def gather_tick(k):
        for s in (5, 4, 3, 2, 1):
            u = k - s + 1

            def step(s=s, u=u):
                if s > 1:
                    for copy in gather_copies(u, s - 1):
                        copy.wait()
                if s < 5:
                    for copy in gather_copies(u, s):
                        copy.start()

            if isinstance(u, int):
                if 0 <= u < units:
                    step()
            else:
                pl.when(jnp.logical_and(u >= 0, u < units))(step)

    def reduce_copies(s):
        st, rc = ((st1, rc1), (st2, rc2), (st3, rc3), (st4, rc4))[s - 1]
        copies = []
        for colour in range(2):
            axis = ("x", "y")[(colour + (s > 2)) % 2]
            for way, sign in ((0, 1), (1, -1)):
                copies.append(
                    pltpu.make_async_remote_copy(
                        src_ref=st.at[colour, way],
                        dst_ref=rc.at[colour, way],
                        send_sem=rs_send.at[s - 1, colour * 2 + way],
                        recv_sem=rs_recv.at[s - 1, colour * 2 + way],
                        device_id={"dp": beside[axis, sign]},
                    )
                )
        return copies

    def part(par, colour, s, k, lo, n):
        axis = ("x", "y")[(colour + (s > 2)) % 2]
        pos = (xs if axis == "x" else ys)[k]
        lanes = pl.ds(colour * half + lo, n)
        if s <= 2:
            i, j = (pos, slice(None)) if axis == "x" else (slice(None), pos)
        else:
            i, j = (pos, py) if axis == "x" else (px, pos)
        return g.at[par, :, i, j, :, lanes]

    def begin(par, s):
        for colour in range(2):
            for way in range(2):
                (st1 if s == 1 else st3)[colour, way] = part(par, colour, s, 2, way * quarter, quarter)[...].astype(BF16)
        for copy in reduce_copies(s):
            copy.start()

    def middle(par, s):
        for copy in reduce_copies(s - 1):
            copy.wait()
        st, rc = (st2, rc1) if s == 2 else (st4, rc3)
        for colour in range(2):
            for way, sign in ((0, 1), (1, -1)):
                took, kept = way * quarter, (1 - way) * quarter
                st[colour, way, ..., pl.ds(took, quarter)] = (
                    part(par, colour, s, sign, took, quarter)[...] + rc[colour, way].astype(F32)
                ).astype(BF16)
                st[colour, way, ..., pl.ds(kept, quarter)] = part(par, colour, s, sign, kept, quarter)[...].astype(BF16)
        for copy in reduce_copies(s):
            copy.start()

    def reduce_tick(n, par, u):
        if n == 1:
            begin(par, 1)
        elif n == 2:
            middle(par, 2)
        elif n == 3:
            for copy in reduce_copies(2):
                copy.wait()
            for colour in range(2):
                own = part(par, colour, 2, 0, 0, half)
                own[...] = own[...] + rc2[colour, 0].astype(F32) + rc2[colour, 1].astype(F32)
            begin(par, 3)
        elif n == 4:
            middle(par, 4)
        else:
            for copy in reduce_copies(4):
                copy.wait()
            for colour in range(2):
                own = part(par, colour, 4, 0, 0, half)[...]
                total = own + rc4[colour, 0].astype(F32) + rc4[colour, 1].astype(F32)
                lanes = pl.ds(colour * half, half)
                fin[u % CHUNKS, :, :, lanes] = total[:2].astype(BF16)
                out_down[u, :, lanes] = total[2].astype(BF16)

    def at(t):
        return pl.ds(pl.multiple_of(t * tile, tile), tile)

    def matrix(u, k):
        return w[u, k].reshape(d, hid)

    def norm(l, t):
        wide = h[l, at(t)].astype(F32)
        scale = lax.rsqrt(jnp.mean(wide * wide, -1, keepdims=True) + EPS)
        a[l, at(t)] = (wide * scale).astype(BF16)

    def loop(n, body):
        lax.fori_loop(0, n, lambda i, c: (body(i), c)[1], 0)

    def keep(i):
        return pltpu.make_async_copy(kept.at[i % 2], kept_hbm.at[i], keep_sem.at[i % 2])

    def fetch(i):
        return pltpu.make_async_copy(kept_hbm.at[i], kept.at[i % 2], keep_sem.at[i % 2])

    def fwd1(i):
        u, t = i // TILES, i % TILES
        rowsa = a[0, at(t)]
        gate = dot(rowsa, matrix(u, 0), 1, 0)
        up = dot(rowsa, matrix(u, 1), 1, 0)
        kept[i % 2, 0] = gate
        kept[i % 2, 1] = up
        s_tile[i % 2, 2] = (gate * jax.nn.sigmoid(gate) * up).astype(BF16)

    def fwd2(i):
        u, t = i // TILES, i % TILES
        new = dot(s_tile[i % 2, 2], matrix(u, 2), 1, 0)
        acc[at(t)] = jnp.where(u == 0, 0.0, acc[at(t)]) + new

    def fwd_end(t):
        first = h[0, at(t)].astype(F32) + acc[at(t)].astype(BF16).astype(F32)
        h[1, at(t)] = first.astype(BF16)
        norm(1, t)

    def bwd1(l, i, late=False):
        u, t = l * CHUNKS + i // TILES, i % TILES
        n = tile // HALVES
        for r in range(HALVES):
            q = pl.ds(r * n, n)
            rr = pl.ds(pl.multiple_of(t * tile + r * n, n), n)
            if l:
                rowsa = a[l, rr]
                gate = dot(rowsa, matrix(u, 0), 1, 0)
                up = dot(rowsa, matrix(u, 1), 1, 0)
            else:
                gate, up = kept[i % 2, 0, q], kept[i % 2, 1, q]
            by = dot(dh[rr], matrix(u, 2), 1, 1).astype(BF16).astype(F32)
            sig = jax.nn.sigmoid(gate)
            silu = gate * sig
            by_gate = (by * up * (sig + silu * (1.0 - sig))).astype(BF16)
            by_up = (by * silu).astype(BF16)
            if late:
                h[1, rr] = by_gate
                a[1, rr] = by_up
            else:
                s_tile[i % 2, 0, q] = by_gate
                s_tile[i % 2, 1, q] = by_up
            s_tile[i % 2, 2, q] = (silu * up).astype(BF16)

    def by_hidden(i, late):
        t = i % TILES
        return (h[1, at(t)], a[1, at(t)]) if late else (s_tile[i % 2, 0], s_tile[i % 2, 1])

    def bwd_in(l, i, late=False):
        chunk, t = i // TILES, i % TILES
        u = l * CHUNKS + chunk
        by_gate, by_up = by_hidden(i, late)
        new = dot(by_gate, matrix(u, 0), 1, 1) + dot(by_up, matrix(u, 1), 1, 1)
        acc[at(t)] = jnp.where(chunk == 0, 0.0, acc[at(t)]) + new

    def bwd_w(l, i, late=False):
        chunk, t = i // TILES, i % TILES
        par = chunk % 2
        by_gate, by_up = by_hidden(i, late)
        rowsa = a[l, at(t)]
        for k, (p, q) in enumerate(((rowsa, by_gate), (rowsa, by_up), (s_tile[i % 2, 2], dh[at(t)]))):
            old = jnp.where(t == 0, 0.0, g[par, k])
            g[par, k] = old + dot(p, q, 0, 0).reshape(old.shape)

    def bwd_end(l, t):
        wide = h[l, at(t)].astype(F32)
        scale = lax.rsqrt(jnp.mean(wide * wide, -1, keepdims=True) + EPS)
        da = acc[at(t)].astype(BF16).astype(F32)
        along = jnp.mean(da * wide, -1, keepdims=True)
        by = (da * scale - wide * (scale * scale * scale * along)).astype(BF16)
        dh[at(t)] = (dh[at(t)].astype(F32) + by.astype(F32)).astype(BF16)

    load_w.wait()
    gather_tick(0)
    gather_tick(1)
    load_x.wait()
    loop(TILES // 2, lambda t: norm(0, t))
    gather_tick(2)
    loop(TILES - TILES // 2, lambda t: norm(0, t + TILES // 2))
    gather_tick(3)
    gather_tick(4)

    steps = CHUNKS * TILES
    fwd1(0)
    keep(0).start()

    def fwd_step(i):
        @pl.when(i % TILES == 0)
        def _():
            gather_tick(4 + i // TILES)

        @pl.when(i >= 2)
        def _():
            keep(i - 2).wait()

        fwd1(i)
        fwd2(i - 1)
        keep(i).start()

    loop(steps - 1, lambda i: fwd_step(i + 1))
    fwd2(steps - 1)
    loop(TILES, fwd_end)
    load_dy.wait()
    gather_tick(4 + CHUNKS)
    for i in (steps - 2, steps - 1):
        keep(i).wait()
    for i in range(2):
        fetch(i).start()

    when = ((1, 1), (2, 3), (3, 5), (4, 6), (5, 7))

    def step1(i):
        chunk, t = i // TILES, i % TILES

        @pl.when(t == 0)
        def _():
            gather_tick(4 + CHUNKS + chunk)

        for tick, place in when:

            @pl.when(jnp.logical_and(t == place, chunk > 0))
            def _(tick=tick):
                reduce_tick(tick, (chunk + 1) % 2, CHUNKS + chunk - 1)

        bwd_w(1, i - 1)
        bwd_in(1, i - 1)
        bwd1(1, i)

    bwd1(1, 0)
    loop(steps - 1, lambda i: step1(i + 1))
    bwd_in(1, steps - 1)
    bwd_w(1, steps - 1)
    loop(TILES, lambda t: bwd_end(1, t))

    def ticks(chunk, t):
        for tick, place in when:

            @pl.when(t == place)
            def _(tick=tick):
                reduce_tick(tick, (chunk + 1) % 2, (chunk + 2 * CHUNKS - 1) % (2 * CHUNKS))
                if tick == 5:
                    pl.when(chunk == 0)(lambda: finish(1))

    def step0(i):
        ticks(i // TILES, i % TILES)
        fetch(i + 1).start()
        fetch(i).wait()
        bwd_w(0, i - 1)
        bwd_in(0, i - 1)
        bwd1(0, i)

    def step0_late(i):
        ticks(i // TILES, i % TILES)
        pl.when(i + 1 < steps)(lambda: fetch(i + 1).start())
        fetch(i).wait()
        bwd1(0, i, True)
        bwd_w(0, i - 1, True)

    fetch(0).wait()
    bwd1(0, 0)
    early = steps - TILES
    loop(early - 1, lambda i: step0(i + 1))
    fetch(early + 1).start()
    fetch(early).wait()
    bwd1(0, early, True)
    bwd_in(0, early - 1)
    bwd_w(0, early - 1)
    loop(TILES - 1, lambda i: step0_late(i + early + 1))
    bwd_w(0, steps - 1, True)

    def end0(t):
        bwd_in(0, early + t, True)
        bwd_end(0, t)

    done = 0
    for tick, share in ((1, 2), (2, 3), (3, 1), (4, 2), (5, 0)):
        reduce_tick(tick, (CHUNKS - 1) % 2, CHUNKS - 1)
        if share:
            loop(share, lambda t, done=done: end0(t + done))
        done += share
        if tick == 4:
            store = pltpu.make_async_copy(dh, dx_hbm, load_sem.at[0])
            store.start()
    finish(0)
    store.wait()


def solution(mesh):
    ways = mesh.shape["dp"]
    side = math.isqrt(ways)

    def step(x, dy, w_gate, w_up, w_down):
        layers, rows, ff = w_gate.shape
        tokens, d = x.shape[1:]
        hid = ff // CHUNKS
        own = w_down.shape[1] // CHUNKS
        assert rows == own and d == hid and layers == 2
        units = layers * CHUNKS

        hbm, vmem = (pl.BlockSpec(memory_space=m) for m in (pl.ANY, pltpu.VMEM))
        tile = tokens // TILES
        quarter, half = hid // 4, hid // 2
        by_x, by_gate, by_up, by_down, _ = pl.pallas_call(
            functools.partial(kernel, side, layers),
            out_shape=(
                jax.ShapeDtypeStruct((tokens, d), BF16),
                jax.ShapeDtypeStruct(w_gate.shape, BF16),
                jax.ShapeDtypeStruct(w_up.shape, BF16),
                jax.ShapeDtypeStruct((units, rows, hid), BF16),
                jax.ShapeDtypeStruct((CHUNKS * TILES, 2, tile, hid), F32),
            ),
            in_specs=[hbm, hbm, vmem, vmem, hbm],
            out_specs=(hbm, vmem, vmem, vmem, hbm),
            scratch_shapes=[
                pltpu.VMEM((units, 3, side, side, rows, hid), BF16),
                pltpu.VMEM((layers, tokens, d), BF16),
                pltpu.VMEM((layers, tokens, d), BF16),
                pltpu.VMEM((tokens, d), BF16),
                pltpu.VMEM((tokens, d), F32),
                pltpu.VMEM((2, 3, side, side, rows, hid), F32),
                pltpu.VMEM((2, 3, tile, hid), BF16),
                pltpu.VMEM((2, 2, tile, hid), F32),
                pltpu.VMEM((hid, hid), BF16),
                pltpu.VMEM((CHUNKS, 2, rows, hid), BF16),
                *[
                    pltpu.VMEM(shape, BF16)
                    for _ in range(2)
                    for shape in (
                        (2, 2, 3, side, rows, quarter),
                        (2, 2, 3, side, rows, half),
                        (2, 2, 3, rows, quarter),
                        (2, 2, 3, rows, half),
                    )
                ],
                pltpu.SemaphoreType.DMA((3,)),
                pltpu.SemaphoreType.DMA((2,)),
                pltpu.SemaphoreType.DMA((units, 4, 4)),
                pltpu.SemaphoreType.DMA((units, 4, 4)),
                pltpu.SemaphoreType.DMA((4, 4)),
                pltpu.SemaphoreType.DMA((4, 4)),
            ],
            compiler_params=pltpu.CompilerParams(
                collective_id=0, has_side_effects=True, vmem_limit_bytes=67_043_328
            ),
        )(x[0], dy[0], w_gate, w_up, w_down.reshape(units, rows, d))

        return by_x[None], by_gate, by_up, by_down.reshape(w_down.shape)

    tok, mat, grad = P(("rep", "dp")), P(None, "dp"), P("rep", "dp")
    return jax.shard_map(
        step,
        mesh=mesh,
        in_specs=(tok, tok, mat, mat, mat),
        out_specs=(tok, grad, grad, grad),
        check_vma=False,
    )
```

time: 804 us -> 282 us (0.35); the launches traced: 795 us -> 281 us
  waiting for transfers between devices: 331 us -> 0 us
  matrix products: 304 us -> 0 us
  Pallas kernels: 0 us -> 274 us
  other arithmetic: 113 us -> 0 us
  local copies, waits for them, and re-layouts: 30.5 us -> 6.66 us
  between operations: 14.8 us -> 0.67 us
    dot_general x17 -> x0, matrix products: 304 us -> none  [the longest x6 131 us: layer(): up = jnp.dot(a, w['w_up'], preferred_element_type=jnp.float32)]
    pallas_call x0 -> x1, Pallas kernels: none -> 274 us  [step(): pl.pallas_call(functools.partial(kernel, side, layers), out_shape=(jax.Sh...]
    unnamed x18 -> x0, waiting for transfers between devices: 242 us -> none
    squeeze x6 -> x0, waiting for transfers between devices: 88.9 us -> none  [stack(): h = layer(h, {name: w[number] for name, w in weights.items()})]
    unnamed x3 -> x0, other arithmetic: 87.4 us -> none
    unnamed x29 -> x10, local copies, waits for them, and re-layouts: 25.5 us -> 6.66 us
    reshape x4 -> x0, other arithmetic: 9.73 us -> none  [the longest x1 7.57 us: step(): by_x.reshape(shape)]
  transfers between devices with their start and end apart: 12 -> 0, of which waited for: 8 -> 0; matrix products, arithmetic and copies ran while one was open for 55% -> 0% of each run, Pallas kernels for 0% -> 0%
where the time goes in v1:
time: 282 us; the launch traced here: 281 us
  Pallas kernels  274 us (97%)
  local copies, waits for them, and re-layouts  6.66 us (2%)
    pallas_call x1, Pallas kernels, step(): pl.pallas_call(functools.partial(kernel, side, layers), out_shape=(jax.Sh...  274 us
    unnamed x10, local copies, waits for them, and re-layouts  6.66 us

profile of v1, /device:TPU:98, one launch (start us, length us, event | category | flops | bytes accessed | tf_op | source)
XLA Modules:
  0.0 281.5 jit_solution(14124963237992255361)
XLA Ops:
  0.6 274.1 %shard_map.84 = (bf16[4096,512]{1,0:T(8,128)(2,1)}, bf16[2,32,2048]{2,1,0:T(8,128)(2,1)}, bf16[2,32,2048]{2,1,0:T(8,128)(2,1)}, bf16[8,32,512]{2,1,0:T(8,128)(2,1)}, f32[32,2,512,512]{3,2,1,0:T(8,128)}) custom-call(bf16[4096,512]{1,0:T(8,128)(2,1)} %bitcast.5, bf16[4096,512]{1,0:T(8,128)(2,1)} %bitcast.6, bf16[2,32,2048]{2,1,0:T(8,128)(2,1)} %gate_own.1, ...), custom_call_target="tpu_custom_call" | custom-call | tf_op jit(solution)/shard_map/pallas_call | solution.py:424
  274.8 0.0 copy-start.2
  274.8 0.0 copy-start.1
  274.8 0.0 copy-start
  274.8 4.5 %copy.13 = bf16[1,4096,512]{2,1,0:T(8,128)(2,1)} copy(bf16[1,4096,512]{2,1,0:T(8,128)(2,1)} %bitcast.7) | data formatting | bytes 8388608
  279.4 0.0 copy-done.2
  279.4 0.7 copy.14
  280.1 0.0 copy-done.1
  280.1 0.7 copy.15
  280.8 0.0 copy-done
  280.8 0.7 copy.16
Async XLA Ops:
  274.8 4.6 %copy-start.2 = (bf16[2,32,2048]{2,1,0:T(8,128)(2,1)S(1)}, bf16[2,32,2048]{2,1,0:T(8,128)(2,1)}, u32[]{:S(2)}) copy-start(bf16[2,32,2048]{2,1,0:T(8,128)(2,1)} %get-tuple-element.17) | copy-start | bytes 786436
  274.8 5.3 %copy-start.1 = (bf16[2,32,2048]{2,1,0:T(8,128)(2,1)S(1)}, bf16[2,32,2048]{2,1,0:T(8,128)(2,1)}, u32[]{:S(2)}) copy-start(bf16[2,32,2048]{2,1,0:T(8,128)(2,1)} %get-tuple-element.18) | copy-start | bytes 786436
  274.8 6.0 %copy-start = (bf16[8,32,512]{2,1,0:T(8,128)(2,1)S(1)}, bf16[8,32,512]{2,1,0:T(8,128)(2,1)}, u32[]{:S(2)}) copy-start(bf16[8,32,512]{2,1,0:T(8,128)(2,1)} %get-tuple-element.11) | copy-start | bytes 786436

commit v2 on v1

--- a/solution.py
+++ b/solution.py
@@ -109,17 +109,20 @@
                 )
         return copies
 
+    def gather_done(u):
+        for copy in gather_copies(u, 4):
+            copy.wait()
+
     def gather_tick(k):
-        for s in (5, 4, 3, 2, 1):
+        for s in (4, 3, 2, 1):
             u = k - s + 1
 
             def step(s=s, u=u):
                 if s > 1:
                     for copy in gather_copies(u, s - 1):
                         copy.wait()
-                if s < 5:
-                    for copy in gather_copies(u, s):
-                        copy.start()
+                for copy in gather_copies(u, s):
+                    copy.start()
 
             if isinstance(u, int):
                 if 0 <= u < units:
@@ -299,7 +302,7 @@
     gather_tick(2)
     loop(TILES - TILES // 2, lambda t: norm(0, t + TILES // 2))
     gather_tick(3)
-    gather_tick(4)
+    gather_done(0)
 
     steps = CHUNKS * TILES
     fwd1(0)
@@ -307,6 +310,10 @@
 
     def fwd_step(i):
         @pl.when(i % TILES == 0)
+        def _():
+            gather_done(i // TILES)
+
+        @pl.when(i % TILES == 2)
         def _():
             gather_tick(4 + i // TILES)
 
@@ -322,7 +329,7 @@
     fwd2(steps - 1)
     loop(TILES, fwd_end)
     load_dy.wait()
-    gather_tick(4 + CHUNKS)
+    gather_done(CHUNKS)
     for i in (steps - 2, steps - 1):
         keep(i).wait()
     for i in range(2):
@@ -334,6 +341,10 @@
         chunk, t = i // TILES, i % TILES
 
         @pl.when(t == 0)
+        def _():
+            gather_done(CHUNKS + chunk)
+
+        @pl.when(t == 2)
         def _():
             gather_tick(4 + CHUNKS + chunk)
 

time: 282 us -> 284 us (level)
  no operation moved by 1% of the time
where the time goes in v2:
time: 284 us; the launch traced here: 283 us
  Pallas kernels  276 us (97%)
  local copies, waits for them, and re-layouts  6.66 us (2%)
    pallas_call x1, Pallas kernels, step(): pl.pallas_call(functools.partial(kernel, side, layers), out_shape=(jax.Sh...  276 us
    unnamed x10, local copies, waits for them, and re-layouts  6.66 us

profile of v2, /device:TPU:98, one launch (start us, length us, event | category | flops | bytes accessed | tf_op | source)
XLA Modules:
  0.0 283.5 jit_solution(93053973366156000)
XLA Ops:
  0.6 276.1 %shard_map.84 = (bf16[4096,512]{1,0:T(8,128)(2,1)}, bf16[2,32,2048]{2,1,0:T(8,128)(2,1)}, bf16[2,32,2048]{2,1,0:T(8,128)(2,1)}, bf16[8,32,512]{2,1,0:T(8,128)(2,1)}, f32[32,2,512,512]{3,2,1,0:T(8,128)}) custom-call(bf16[4096,512]{1,0:T(8,128)(2,1)} %bitcast.5, bf16[4096,512]{1,0:T(8,128)(2,1)} %bitcast.6, bf16[2,32,2048]{2,1,0:T(8,128)(2,1)} %gate_own.1, ...), custom_call_target="tpu_custom_call" | custom-call | tf_op jit(solution)/shard_map/pallas_call | solution.py:435
  276.8 0.0 copy-start.2
  276.8 0.0 copy-start.1
  276.8 0.0 copy-start
  276.8 4.5 %copy.13 = bf16[1,4096,512]{2,1,0:T(8,128)(2,1)} copy(bf16[1,4096,512]{2,1,0:T(8,128)(2,1)} %bitcast.7) | data formatting | bytes 8388608
  281.3 0.0 copy-done.2
  281.3 0.7 copy.14
  282.0 0.0 copy-done.1
  282.0 0.7 copy.15
  282.7 0.0 copy-done
  282.7 0.7 copy.16
Async XLA Ops:
  276.8 4.6 %copy-start.2 = (bf16[2,32,2048]{2,1,0:T(8,128)(2,1)S(1)}, bf16[2,32,2048]{2,1,0:T(8,128)(2,1)}, u32[]{:S(2)}) copy-start(bf16[2,32,2048]{2,1,0:T(8,128)(2,1)} %get-tuple-element.17) | copy-start | bytes 786436
  276.8 5.3 %copy-start.1 = (bf16[2,32,2048]{2,1,0:T(8,128)(2,1)S(1)}, bf16[2,32,2048]{2,1,0:T(8,128)(2,1)}, u32[]{:S(2)}) copy-start(bf16[2,32,2048]{2,1,0:T(8,128)(2,1)} %get-tuple-element.18) | copy-start | bytes 786436
  276.8 6.0 %copy-start = (bf16[8,32,512]{2,1,0:T(8,128)(2,1)S(1)}, bf16[8,32,512]{2,1,0:T(8,128)(2,1)}, u32[]{:S(2)}) copy-start(bf16[8,32,512]{2,1,0:T(8,128)(2,1)} %get-tuple-element.11) | copy-start | bytes 786436
